TPU v7x, 128 devices: a whole 4x4x4 slice. The times are simulated.
128 devices in a mesh: beta: 64 (over z, y, x), grp: 2 (over core).
Axes of the slice: x: 4, y: 4, z: 4, core: 2. Of those that a mesh axis runs over, the one named last changes fastest.
Arguments:
- samples: float32 [128, 8, 128, 128], P('beta', 'grp'), parts along dimension 1, may hold values from -6 to 6
Outputs:
- coeffs: float32 [128, 2, 8, 64, 64], P('beta', None, 'grp'), parts along dimension 2
- power: float32 [8, 64], P('grp'), parts along dimension 0
There are 2 independent parts, one for each index of `grp`. A program takes and returns all parts, laid end to end along the dimension named above; each array names one. Nothing has to cross between parts.
All inputs are finite; a program needn't handle non-finite values.
Results may differ from a plain program's by a relative error of at most 0.0003.
Values sent between devices are 32-bit elements; how exact they have to be, the bound alone decides.
A program may use at most 64 MiB of HBM per device.

v0:
```python
import jax
import jax.numpy as jnp
from jax import lax
from jax.sharding import PartitionSpec as P

HIGHEST = lax.Precision.HIGHEST


def swapped(value, axis, apart):
    mask = 2**apart
    pairs = [(source, source ^ mask) for source in range(lax.axis_size(axis))]
    return lax.ppermute(value, axis, pairs)


def from_everyone(shard, axis):
    peers = lax.axis_size(axis)
    return lax.all_to_all(
        jnp.broadcast_to(shard[None], (peers, *shard.shape)), axis, 0, 0, tiled=True
    )


def taken_together(shard, axis):
    return from_everyone(shard, axis).sum(axis=0)


def beta_angles(spread):
    grid_size = 2 * spread
    return (2.0 * jnp.arange(grid_size, dtype=jnp.float32) + 1.0) * (jnp.pi / (4.0 * spread))


def quadrature(spread):
    angles = beta_angles(spread)
    odd_terms = 2.0 * jnp.arange(spread, dtype=jnp.float32) + 1.0
    series = jnp.sum(jnp.sin(angles[:, None] * odd_terms[None, :]) / odd_terms[None, :], axis=1)
    return 2.0 / spread * jnp.sin(angles) * series


def gamma_table(spread):
    grid_size = 2 * spread
    positions = jnp.arange(grid_size, dtype=jnp.int32)
    orders = jnp.arange(spread, dtype=jnp.int32)
    phase_index = positions[:, None] * orders[None, :] % grid_size
    angles = phase_index.astype(jnp.float32) * (2.0 * jnp.pi / grid_size)
    return jnp.concatenate([jnp.cos(angles), -jnp.sin(angles)], axis=1)


def alpha_table(spread, row_index):
    grid_size = 2 * spread
    positions = jnp.arange(grid_size, dtype=jnp.int32)
    phase_index = row_index[:, None] * positions[None, :] % grid_size
    angles = phase_index.astype(jnp.float32) * (2.0 * jnp.pi / grid_size)
    cosine = jnp.cos(angles) / grid_size
    sine_part = jnp.sin(angles) / grid_size
    real_rows = jnp.stack([cosine, sine_part], axis=1)
    imag_rows = jnp.stack([-sine_part, cosine], axis=1)
    return jnp.stack([real_rows, imag_rows], axis=0)


def log_factorial(value, float_type):
    return lax.lgamma((value + 1).astype(float_type))


def wigner_start(alpha_order, gamma_order, log_cosine, log_sine):
    float_type = log_cosine.dtype
    lowest = jnp.maximum(jnp.abs(alpha_order), gamma_order)
    shift_low = jnp.maximum(0, gamma_order - alpha_order)
    magnitude = 0.5 * (
        log_factorial(lowest + alpha_order, float_type)
        + log_factorial(lowest - alpha_order, float_type)
        + log_factorial(lowest + gamma_order, float_type)
        + log_factorial(lowest - gamma_order, float_type)
    )
    magnitude = (
        magnitude
        - log_factorial(lowest + gamma_order - shift_low, float_type)
        - log_factorial(shift_low, float_type)
    )
    magnitude = magnitude - log_factorial(alpha_order - gamma_order + shift_low, float_type)
    magnitude = magnitude - log_factorial(lowest - alpha_order - shift_low, float_type)
    cos_power = (2 * lowest + gamma_order - alpha_order - 2 * shift_low).astype(float_type)
    sin_power = (alpha_order - gamma_order + 2 * shift_low).astype(float_type)
    parity = (alpha_order - gamma_order + shift_low) % 2
    sign_factor = (1 - 2 * parity).astype(float_type)
    return sign_factor * jnp.exp(magnitude + cos_power * log_cosine + sin_power * log_sine)


def advance(degree, carried, alpha_order, gamma_order, cos_angles, start_value, lowest):
    former, current = carried
    float_type = current.dtype
    previous = (degree - 1).astype(float_type)
    alpha_float = alpha_order.astype(float_type)
    gamma_float = gamma_order.astype(float_type)
    cross_ratio = alpha_float * gamma_float / jnp.maximum(previous * (previous + 1.0), 1.0)
    upper_term = ((previous + 1.0) * (previous + 1.0) - alpha_float * alpha_float) * (
        (previous + 1.0) * (previous + 1.0) - gamma_float * gamma_float
    )
    lower_term = (previous * previous - alpha_float * alpha_float) * (
        previous * previous - gamma_float * gamma_float
    )
    root_upper = jnp.sqrt(jnp.maximum(upper_term, 1.0))
    forward = (previous + 1.0) * (2.0 * previous + 1.0) / root_upper
    backward = (
        (previous + 1.0)
        * jnp.sqrt(jnp.maximum(lower_term, 0.0))
        / (jnp.maximum(previous, 1.0) * root_upper)
    )
    recurred = forward * (cos_angles - cross_ratio) * current - backward * former
    renewed = jnp.where(degree == lowest, start_value, recurred)
    return (current, renewed)


def degree_rows(row_index, weighted, spread):
    stride = 8
    grid_size = 2 * spread
    group_size = row_index.shape[0]
    channels = weighted.shape[2]
    block_count = spread // stride
    alpha_order = jnp.where(row_index < spread, row_index, row_index - grid_size)[:, None, None]
    gamma_order = jnp.arange(spread, dtype=jnp.int32)[None, None, :]
    angles = beta_angles(spread)
    cos_angles = jnp.cos(angles)[None, :, None]
    log_cosine = jnp.log(jnp.cos(0.5 * angles))[None, :, None]
    log_sine = jnp.log(jnp.sin(0.5 * angles))[None, :, None]
    lowest = jnp.maximum(jnp.abs(alpha_order), gamma_order)
    start_value = wigner_start(alpha_order, gamma_order, log_cosine, log_sine)
    first_block = jnp.min(jnp.abs(alpha_order)) // stride
    empty_state = jnp.zeros((group_size, grid_size, spread), jnp.float32)

    def compute_block(operands):
        block_index, former, current = operands
        levels = []
        for offset in range(stride):
            former, current = advance(
                block_index * stride + offset,
                (former, current),
                alpha_order,
                gamma_order,
                cos_angles,
                start_value,
                lowest,
            )
            levels.append(current)
        stacked = jnp.stack(levels, axis=0)
        block_part = jnp.einsum("jgkq,kgcq->gcjq", stacked, weighted, precision=HIGHEST)
        return (former, current, block_part)

    def skip_block(operands):
        block_index, former, current = operands
        return (former, current, jnp.zeros((group_size, channels, stride, spread), jnp.float32))

    def block_step(carried, block_index):
        former, current = carried
        former, current, block_part = lax.cond(
            block_index >= first_block, compute_block, skip_block, (block_index, former, current)
        )
        return ((former, current), block_part)

    _, parts = lax.scan(
        block_step, (empty_state, empty_state), jnp.arange(block_count, dtype=jnp.int32)
    )
    output = jnp.transpose(parts, (1, 2, 0, 3, 4)).reshape(group_size, channels, spread, spread)
    degree_scale = 8.0 * jnp.sqrt(2.0 * jnp.arange(spread, dtype=jnp.float32) + 1.0)
    return output * degree_scale[None, None, :, None]


def degree_energy(coeffs, functions, spread):
    split_view = coeffs.reshape(coeffs.shape[0], 2, functions, spread, spread)
    multiplicity = jnp.where(jnp.arange(spread) == 0, 1.0, 2.0).astype(jnp.float32)
    energy_sum = jnp.sum(split_view * split_view * multiplicity, axis=(0, 1, 4))
    degrees = 2.0 * jnp.arange(spread, dtype=jnp.float32) + 1.0
    return energy_sum / (degrees * degrees)[None, :]


def local(samples):
    devices = lax.axis_size("beta")
    device = lax.axis_index("beta")
    local_beta = samples.shape[0]
    functions = samples.shape[1]
    grid_size = samples.shape[2]
    spread = grid_size // 2
    channels = 2 * functions
    row_count = grid_size // devices
    natural_rows = jnp.arange(grid_size, dtype=jnp.int32)
    folded = natural_rows.reshape(2, devices // 2, row_count // 2, 2)
    row_order = jnp.stack([folded[:, :, :, 0], folded[::-1, :, :, 1]], axis=3).reshape(grid_size)
    halfway = jnp.einsum("kfag,gx->kfax", samples, gamma_table(spread), precision=HIGHEST)
    halfway = halfway.reshape(local_beta, functions, grid_size, 2, spread)
    spectrum = jnp.einsum(
        "kfacq,spca->kpsfq", halfway, alpha_table(spread, row_order), precision=HIGHEST
    )
    spectrum = spectrum.reshape(local_beta, grid_size, channels, spread)
    received = lax.all_to_all(spectrum, "beta", split_axis=1, concat_axis=0, tiled=True)
    weighted = received * quadrature(spread)[:, None, None, None]
    owned_rows = lax.dynamic_slice_in_dim(row_order, device * row_count, row_count)
    computed = degree_rows(owned_rows, weighted, spread)
    power_part = degree_energy(computed, functions, spread)
    kept = computed[0::2]
    lent = computed[1::2]
    returned = swapped(lent, "beta", devices.bit_length() - 2)
    coeffs = jnp.stack([kept, returned], axis=1).reshape(row_count, channels, spread, spread)
    power = taken_together(power_part, "beta")
    coeffs = coeffs.reshape(row_count, 2, functions, spread, spread)
    return (coeffs, power)


def solution(mesh):
    return jax.shard_map(
        local,
        mesh=mesh,
        in_specs=(P("beta", "grp", None, None),),
        out_specs=(P("beta", None, "grp", None, None), P("grp", None)),
        check_vma=False,
    )
```

profile of v0, /device:TPU:0, one launch (start us, length us, event | category | flops | bytes accessed | tf_op | source)
XLA Modules:
  0.0 99.0 jit_solution(18264558040937235246)
XLA Ops:
  3.5 1.4 %reshape.2616 = f32[64,1,2048]{2,1,0:T(1,128)} reshape(f32[128,2,8,64]{3,2,1,0:T(8,128)S(1)} %bitcast.243) | data formatting | bytes 1048576
  4.9 11.5 %all-to-all-start = ((f32[64,1,2048]{2,1,0:T(1,128)}), f32[64,1,2048]{2,1,0:T(1,128)S(1)}, u32[]{:S(2)}, u32[]{:S(2)}) async-start(f32[64,1,2048]{2,1,0:T(1,128)} %reshape.2616), calls=%async_computation | async-start | bytes 1048576 | tf_op jit(solution)/shard_map/all_to_all | solution.py:192
  20.5 9.3 %all-to-all-done = f32[64,1,2048]{2,1,0:T(1,128)S(1)} async-done(((f32[64,1,2048]{2,1,0:T(1,128)}), f32[64,1,2048]{2,1,0:T(1,128)S(1)}, u32[]{:S(2)}, u32[]{:S(2)}) %all-to-all-start) | async-done | bytes 524320 | tf_op jit(solution)/shard_map/all_to_all | solution.py:192
  30.3 1.9 %reduce.3 = f32[64,2048]{1,0:T(8,128)S(1)} reduce(f32[64,1,2048]{2,1,0:T(1,128)S(1)} %all-to-all-done, f32[]{:T(128)} %broadcast.2750), dimensions={1}, to_apply=%all_to_all.16.reduce_sub_computation | reduce | bytes 1048580 | tf_op jit(solution)/shard_map/all_to_all | solution.py:192
  33.4 46.3 %while.16 = (s32[]{:T(128)}, f32[2,128,64]{1,2,0:T(8,128)S(1)}, f32[2,128,64]{1,2,0:T(8,128)S(1)}, f32[8,2,8,8,64]{4,3,0,2,1:T(8,128)S(1)}, s32[8]{0:T(128)S(1)}...) while((s32[]{:T(128)}, f32[2,128,64]{1,2,0:T(8,128)S(1)}, ...), condition=%wide.region_5.6_spmd.clone.clone, body=%wide.region_2.5_spmd.clone.clone.sunk | while | flops 13465411 | bytes 3031079 | solution.py:158
  34.6 4.4 %conditional.4 = (f32[2,128,64]{1,2,0:T(8,128)S(1)}, f32[2,128,64]{1,2,0:T(8,128)S(1)}, f32[1,2,8,8,64]{2,3,4,1,0:T(8,128)S(1)}) conditional(s32[]{:T(128)} %convert_element_type.314, (f32[2,128,64]{1,2,0:T(8,128)S(1)}, f32[2,128,64]{1,2,0:T(8,128)S(1)}) %tuple.142, (s32[]{:T(128)}, s32[2]{0:T(128)S(1)}, s32[2,1,1]{0,2,1:T(1,128)S(1)}, ...), branch_computations={%region_3.3_spmd, %region_4.4_spmd.clone} | conditional | flops 13465407 | bytes 2832748 | solution.py:153
  37.2 0.8 stack.67
  38.0 1.0 convolution_bitcast_fusion
  40.4 4.4 %conditional.4 = (f32[2,128,64]{1,2,0:T(8,128)S(1)}, f32[2,128,64]{1,2,0:T(8,128)S(1)}, f32[1,2,8,8,64]{2,3,4,1,0:T(8,128)S(1)}) conditional(s32[]{:T(128)} %convert_element_type.314, (f32[2,128,64]{1,2,0:T(8,128)S(1)}, f32[2,128,64]{1,2,0:T(8,128)S(1)}) %tuple.142, (s32[]{:T(128)}, s32[2]{0:T(128)S(1)}, s32[2,1,1]{0,2,1:T(1,128)S(1)}, ...), branch_computations={%region_3.3_spmd, %region_4.4_spmd.clone} | conditional | flops 13465407 | bytes 2832748 | solution.py:153
  43.0 0.8 stack.67
  43.8 1.0 convolution_bitcast_fusion
  46.2 4.4 %conditional.4 = (f32[2,128,64]{1,2,0:T(8,128)S(1)}, f32[2,128,64]{1,2,0:T(8,128)S(1)}, f32[1,2,8,8,64]{2,3,4,1,0:T(8,128)S(1)}) conditional(s32[]{:T(128)} %convert_element_type.314, (f32[2,128,64]{1,2,0:T(8,128)S(1)}, f32[2,128,64]{1,2,0:T(8,128)S(1)}) %tuple.142, (s32[]{:T(128)}, s32[2]{0:T(128)S(1)}, s32[2,1,1]{0,2,1:T(1,128)S(1)}, ...), branch_computations={%region_3.3_spmd, %region_4.4_spmd.clone} | conditional | flops 13465407 | bytes 2832748 | solution.py:153
  48.8 0.8 stack.67
  49.6 1.0 convolution_bitcast_fusion
  52.0 4.4 %conditional.4 = (f32[2,128,64]{1,2,0:T(8,128)S(1)}, f32[2,128,64]{1,2,0:T(8,128)S(1)}, f32[1,2,8,8,64]{2,3,4,1,0:T(8,128)S(1)}) conditional(s32[]{:T(128)} %convert_element_type.314, (f32[2,128,64]{1,2,0:T(8,128)S(1)}, f32[2,128,64]{1,2,0:T(8,128)S(1)}) %tuple.142, (s32[]{:T(128)}, s32[2]{0:T(128)S(1)}, s32[2,1,1]{0,2,1:T(1,128)S(1)}, ...), branch_computations={%region_3.3_spmd, %region_4.4_spmd.clone} | conditional | flops 13465407 | bytes 2832748 | solution.py:153
  54.6 0.8 stack.67
  55.4 1.0 convolution_bitcast_fusion
  57.7 4.4 %conditional.4 = (f32[2,128,64]{1,2,0:T(8,128)S(1)}, f32[2,128,64]{1,2,0:T(8,128)S(1)}, f32[1,2,8,8,64]{2,3,4,1,0:T(8,128)S(1)}) conditional(s32[]{:T(128)} %convert_element_type.314, (f32[2,128,64]{1,2,0:T(8,128)S(1)}, f32[2,128,64]{1,2,0:T(8,128)S(1)}) %tuple.142, (s32[]{:T(128)}, s32[2]{0:T(128)S(1)}, s32[2,1,1]{0,2,1:T(1,128)S(1)}, ...), branch_computations={%region_3.3_spmd, %region_4.4_spmd.clone} | conditional | flops 13465407 | bytes 2832748 | solution.py:153
  60.4 0.8 stack.67
  61.2 1.0 convolution_bitcast_fusion
  63.5 4.4 %conditional.4 = (f32[2,128,64]{1,2,0:T(8,128)S(1)}, f32[2,128,64]{1,2,0:T(8,128)S(1)}, f32[1,2,8,8,64]{2,3,4,1,0:T(8,128)S(1)}) conditional(s32[]{:T(128)} %convert_element_type.314, (f32[2,128,64]{1,2,0:T(8,128)S(1)}, f32[2,128,64]{1,2,0:T(8,128)S(1)}) %tuple.142, (s32[]{:T(128)}, s32[2]{0:T(128)S(1)}, s32[2,1,1]{0,2,1:T(1,128)S(1)}, ...), branch_computations={%region_3.3_spmd, %region_4.4_spmd.clone} | conditional | flops 13465407 | bytes 2832748 | solution.py:153
  66.2 0.8 stack.67
  67.0 1.0 convolution_bitcast_fusion
  69.3 4.4 %conditional.4 = (f32[2,128,64]{1,2,0:T(8,128)S(1)}, f32[2,128,64]{1,2,0:T(8,128)S(1)}, f32[1,2,8,8,64]{2,3,4,1,0:T(8,128)S(1)}) conditional(s32[]{:T(128)} %convert_element_type.314, (f32[2,128,64]{1,2,0:T(8,128)S(1)}, f32[2,128,64]{1,2,0:T(8,128)S(1)}) %tuple.142, (s32[]{:T(128)}, s32[2]{0:T(128)S(1)}, s32[2,1,1]{0,2,1:T(1,128)S(1)}, ...), branch_computations={%region_3.3_spmd, %region_4.4_spmd.clone} | conditional | flops 13465407 | bytes 2832748 | solution.py:153
  71.9 0.8 stack.67
  72.8 1.0 convolution_bitcast_fusion
  75.1 4.4 %conditional.4 = (f32[2,128,64]{1,2,0:T(8,128)S(1)}, f32[2,128,64]{1,2,0:T(8,128)S(1)}, f32[1,2,8,8,64]{2,3,4,1,0:T(8,128)S(1)}) conditional(s32[]{:T(128)} %convert_element_type.314, (f32[2,128,64]{1,2,0:T(8,128)S(1)}, f32[2,128,64]{1,2,0:T(8,128)S(1)}) %tuple.142, (s32[]{:T(128)}, s32[2]{0:T(128)S(1)}, s32[2,1,1]{0,2,1:T(1,128)S(1)}, ...), branch_computations={%region_3.3_spmd, %region_4.4_spmd.clone} | conditional | flops 13465407 | bytes 2832748 | solution.py:153
  77.7 0.8 stack.67
  78.6 1.0 convolution_bitcast_fusion
  81.2 15.4 %all_to_all.23 = f32[64,1,256]{2,1,0:T(1,128)S(1)} all-to-all(f32[64,1,256]{2,1,0:T(1,128)S(1)} %reshape.2618), channel_id=1, replica_groups=mesh['beta'=64,'grp'=2] {'beta'}, dimensions={0} | all-to-all | bytes 131072 | tf_op jit(solution)/shard_map/all_to_all | solution.py:17
  96.6 0.8 reduce.4
  98.2 0.8 pad_maximum_fusion
  (289 shorter events, 28.3 us)
Async XLA Ops:
  0.6 1.0 %copy-start = (f32[2,4,128,128]{3,2,1,0:T(8,128)S(1)}, f32[2,4,128,128]{3,2,1,0:T(8,128)}, u32[]{:S(2)}) copy-start(f32[2,4,128,128]{3,2,1,0:T(8,128)} %param.5) | copy-start | bytes 1572868
  4.9 24.9 %all-to-all-start = ((f32[64,1,2048]{2,1,0:T(1,128)}), f32[64,1,2048]{2,1,0:T(1,128)S(1)}, u32[]{:S(2)}, u32[]{:S(2)}) async-start(f32[64,1,2048]{2,1,0:T(1,128)} %reshape.2616), calls=%async_computation | async-start | bytes 1048576 | tf_op jit(solution)/shard_map/all_to_all | solution.py:192
  80.0 18.2 %collective-permute-start = (f32[1,8,64,64]{3,2,1,0:T(8,128)S(1)}, f32[1,8,64,64]{3,2,1,0:T(8,128)S(1)}, u32[]{:S(2)}, u32[]{:S(2)}) collective-permute-start(f32[1,8,64,64]{3,2,1,0:T(8,128)S(1)} %get-tuple-element.575), channel_id=1, source_target_pairs={{0,64},{2,66},{4,68},{6,70},{8,72},{10,74},{12,76},{14,78},{16,80}... | collective-permute-start | bytes 393224 | tf_op jit(solution)/shard_map/ppermute | solution.py:12
where the time goes:
time: 99.5 us; the launch traced here: 99 us
  other arithmetic  20.7 us (21%)
  local copies, waits for them, and re-layouts  17.3 us (17%)
  blocking collectives  15.4 us (15%)
  starting transfers between devices  12.2 us (12%)
  loops' own time  11.7 us (12%)
  waiting for transfers between devices  9.26 us (9%)
  matrix products  8.89 us (9%)
  between operations  3.47 us (3%)
    all_to_all x1, blocking collectives, from_everyone(): lax.all_to_all(jnp.broadcast_to(shard[None], (peers, *shard.shape)), axis...  15.4 us
    all_to_all x1, starting transfers between devices, local(): lax.all_to_all(spectrum, 'beta', split_axis=1, concat_axis=0, tiled=True)  11.5 us
    all_to_all x1, waiting for transfers between devices, local(): lax.all_to_all(spectrum, 'beta', split_axis=1, concat_axis=0, tiled=True)  9.26 us
    dot_general x8, matrix products, compute_block(): jnp.einsum('jgkq,kgcq->gcjq', stacked, weighted, precision=HIGHEST)  7.68 us
    another operation x8, loops' own time, block_step(): lax.cond(block_index >= first_block, compute_block, skip_block, (block_in...  7.04 us
    another operation x8, local copies, waits for them, and re-layouts, compute_block(): stacked = jnp.stack(levels, axis=0)  6.64 us
    select_n x8, other arithmetic, advance(): renewed = jnp.where(degree == lowest, start_value, recurred)  6.16 us
    div x64, other arithmetic, advance(): forward = (previous + 1.0) * (2.0 * previous + 1.0) / root_upper  5.32 us
  transfers between devices with their start and end apart: 2, of which 1 were waited for; matrix products, arithmetic and copies ran while one was open for 4% of the time, Pallas kernels for 0%

commit v1 on v0

--- a/solution.py
+++ b/solution.py
@@ -4,6 +4,12 @@
 from jax.sharding import PartitionSpec as P
 
 HIGHEST = lax.Precision.HIGHEST
+
+
+def stacked_exchange(shard, axis, split, join):
+    pieces = jnp.split(shard, lax.axis_size(axis), axis=split)
+    arrived = lax.all_to_all(jnp.stack(pieces), axis, 0, 0)
+    return jnp.concatenate(arrived, axis=join)
 
 
 def swapped(value, axis, apart):
@@ -189,7 +195,7 @@
         "kfacq,spca->kpsfq", halfway, alpha_table(spread, row_order), precision=HIGHEST
     )
     spectrum = spectrum.reshape(local_beta, grid_size, channels, spread)
-    received = lax.all_to_all(spectrum, "beta", split_axis=1, concat_axis=0, tiled=True)
+    received = stacked_exchange(spectrum, "beta", 1, 0)
     weighted = received * quadrature(spread)[:, None, None, None]
     owned_rows = lax.dynamic_slice_in_dim(row_order, device * row_count, row_count)
     computed = degree_rows(owned_rows, weighted, spread)

time: 99.5 us -> 197 us (1.98); the launches traced: 99 us -> 193 us
  local copies, waits for them, and re-layouts: 17.3 us -> 111 us
    another operation x0 -> x69, local copies, waits for them, and re-layouts: none -> 57.8 us  [stacked_exchange(): arrived = lax.all_to_all(jnp.stack(pieces), axis, 0, 0)]
    unnamed x7 -> x262, local copies, waits for them, and re-layouts: 2.82 us -> 38.7 us
  transfers between devices with their start and end apart: 2 -> 2, of which waited for: 1 -> 1; matrix products, arithmetic and copies ran while one was open for 4% -> 2% of each run, Pallas kernels for 0% -> 0%
where the time goes in v1:
time: 197 us; the launch traced here: 193 us
  local copies, waits for them, and re-layouts  111 us (56%)
  other arithmetic  20.7 us (11%)
  blocking collectives  15.4 us (8%)
  loops' own time  12.8 us (6%)
  starting transfers between devices  12.5 us (6%)
  matrix products  8.89 us (5%)
  waiting for transfers between devices  8.87 us (5%)
  between operations  3.45 us (2%)
    another operation x69, local copies, waits for them, and re-layouts, stacked_exchange(): arrived = lax.all_to_all(jnp.stack(pieces), axis, 0, 0)  57.8 us
    unnamed x262, local copies, waits for them, and re-layouts  38.7 us
    all_to_all x1, blocking collectives, from_everyone(): lax.all_to_all(jnp.broadcast_to(shard[None], (peers, *shard.shape)), axis...  15.4 us
    all_to_all x1, starting transfers between devices, stacked_exchange(): arrived = lax.all_to_all(jnp.stack(pieces), axis, 0, 0)  11.7 us
    all_to_all x1, waiting for transfers between devices, stacked_exchange(): arrived = lax.all_to_all(jnp.stack(pieces), axis, 0, 0)  8.86 us
    dot_general x8, matrix products, compute_block(): jnp.einsum('jgkq,kgcq->gcjq', stacked, weighted, precision=HIGHEST)  7.68 us
    another operation x8, loops' own time, block_step(): lax.cond(block_index >= first_block, compute_block, skip_block, (block_in...  7.59 us
    another operation x8, local copies, waits for them, and re-layouts, compute_block(): stacked = jnp.stack(levels, axis=0)  6.64 us
  transfers between devices with their start and end apart: 2, of which 1 were waited for; matrix products, arithmetic and copies ran while one was open for 2% of the time, Pallas kernels for 0%

profile of v1, /device:TPU:0, one launch (start us, length us, event | category | flops | bytes accessed | tf_op | source)
XLA Modules:
  0.0 193.3 jit_solution(17235466490859856298)
XLA Ops:
  2.9 1.8 slice_bitcast_fusion.57
  4.7 6.3 %slice_bitcast_fusion.38 = (f32[1,2,2,8,64]{2,4,3,1,0:T(8,128)}, f32[1,2,2,8,64]{2,4,3,1,0:T(8,128)}, f32[1,2,2,8,64]{2,4,3,1,0:T(8,128)}, f32[1,2,2,8,64]{2,4,3...) fusion(f32[2,128,8,64]{1,3,2,0:T(8,128)S(1)} %bitcast.359), kind=kLoop, calls=%fused_computation.138 | loop fusion | bytes 311296 | tf_op jit(solution)/shard_map/stack | solution.py:11
  11.0 6.4 %slice_bitcast_fusion.19 = (f32[1,2,2,8,64]{2,4,3,1,0:T(8,128)}, f32[1,2,2,8,64]{2,4,3,1,0:T(8,128)}, f32[1,2,2,8,64]{2,4,3,1,0:T(8,128)}, f32[1,2,2,8,64]{2,4,3...) fusion(f32[2,128,8,64]{1,3,2,0:T(8,128)S(1)} %bitcast.360), kind=kLoop, calls=%fused_computation.119 | loop fusion | bytes 311296 | tf_op jit(solution)/shard_map/stack | solution.py:11
  17.4 6.3 %slice_bitcast_fusion = (f32[1,2,2,8,64]{2,4,3,1,0:T(8,128)}, f32[1,2,2,8,64]{2,4,3,1,0:T(8,128)}, f32[1,2,2,8,64]{2,4,3,1,0:T(8,128)}, f32[1,2,2,8,64]{2,4,3,1,...) fusion(f32[2,128,8,64]{1,3,2,0:T(8,128)S(1)} %bitcast.361), kind=kLoop, calls=%fused_computation.100 | loop fusion | bytes 311296 | tf_op jit(solution)/shard_map/stack | solution.py:11
  23.7 1.2 copy.243
  25.6 1.8 copy.244
  48.6 1.0 copy.271
  96.4 1.4 reshape.2620
  97.8 11.7 %all-to-all-start = ((f32[64,1,2048]{2,1,0:T(1,128)}), f32[64,1,2048]{2,1,0:T(1,128)S(1)}, u32[]{:S(2)}, u32[]{:S(2)}) async-start(f32[64,1,2048]{2,1,0:T(1,128)} %reshape.2620), calls=%async_computation | async-start | bytes 1048576 | tf_op jit(solution)/shard_map/all_to_all | solution.py:11
  113.9 8.9 %all-to-all-done = f32[64,1,2048]{2,1,0:T(1,128)S(1)} async-done(((f32[64,1,2048]{2,1,0:T(1,128)}), f32[64,1,2048]{2,1,0:T(1,128)S(1)}, u32[]{:S(2)}, u32[]{:S(2)}) %all-to-all-start) | async-done | bytes 524320 | tf_op jit(solution)/shard_map/all_to_all | solution.py:11
  123.2 1.9 reduce.3
  126.3 47.7 %while.16 = (s32[]{:T(128)}, f32[2,128,64]{1,2,0:T(8,128)S(1)}, f32[2,128,64]{1,2,0:T(8,128)S(1)}, f32[8,2,8,8,64]{4,3,0,2,1:T(8,128)S(1)}, s32[8]{0:T(128)S(1)}...) while((s32[]{:T(128)}, f32[2,128,64]{1,2,0:T(8,128)S(1)}, ...), condition=%wide.region_5.6_spmd.clone.clone, body=%wide.region_2.5_spmd.clone.clone.sunk | while | flops 13465411 | bytes 3031079 | solution.py:164
  127.5 4.5 %conditional.4 = (f32[2,128,64]{1,2,0:T(8,128)S(1)}, f32[2,128,64]{1,2,0:T(8,128)S(1)}, f32[1,2,8,8,64]{2,3,4,1,0:T(8,128)S(1)}) conditional(s32[]{:T(128)} %convert_element_type.314, (f32[2,128,64]{1,2,0:T(8,128)S(1)}, f32[2,128,64]{1,2,0:T(8,128)S(1)}) %tuple.202, (s32[]{:T(128)}, s32[2]{0:T(128)S(1)}, s32[2,1,1]{0,2,1:T(1,128)S(1)}, ...), branch_computations={%region_3.3_spmd, %region_4.4_spmd.clone} | conditional | flops 13465407 | bytes 2832748 | solution.py:159
  130.2 0.8 stack.327
  131.1 1.0 convolution_bitcast_fusion
  133.5 4.5 %conditional.4 = (f32[2,128,64]{1,2,0:T(8,128)S(1)}, f32[2,128,64]{1,2,0:T(8,128)S(1)}, f32[1,2,8,8,64]{2,3,4,1,0:T(8,128)S(1)}) conditional(s32[]{:T(128)} %convert_element_type.314, (f32[2,128,64]{1,2,0:T(8,128)S(1)}, f32[2,128,64]{1,2,0:T(8,128)S(1)}) %tuple.202, (s32[]{:T(128)}, s32[2]{0:T(128)S(1)}, s32[2,1,1]{0,2,1:T(1,128)S(1)}, ...), branch_computations={%region_3.3_spmd, %region_4.4_spmd.clone} | conditional | flops 13465407 | bytes 2832748 | solution.py:159
  136.2 0.8 stack.327
  137.0 1.0 convolution_bitcast_fusion
  139.5 4.5 %conditional.4 = (f32[2,128,64]{1,2,0:T(8,128)S(1)}, f32[2,128,64]{1,2,0:T(8,128)S(1)}, f32[1,2,8,8,64]{2,3,4,1,0:T(8,128)S(1)}) conditional(s32[]{:T(128)} %convert_element_type.314, (f32[2,128,64]{1,2,0:T(8,128)S(1)}, f32[2,128,64]{1,2,0:T(8,128)S(1)}) %tuple.202, (s32[]{:T(128)}, s32[2]{0:T(128)S(1)}, s32[2,1,1]{0,2,1:T(1,128)S(1)}, ...), branch_computations={%region_3.3_spmd, %region_4.4_spmd.clone} | conditional | flops 13465407 | bytes 2832748 | solution.py:159
  143.0 1.0 convolution_bitcast_fusion
  145.4 4.5 %conditional.4 = (f32[2,128,64]{1,2,0:T(8,128)S(1)}, f32[2,128,64]{1,2,0:T(8,128)S(1)}, f32[1,2,8,8,64]{2,3,4,1,0:T(8,128)S(1)}) conditional(s32[]{:T(128)} %convert_element_type.314, (f32[2,128,64]{1,2,0:T(8,128)S(1)}, f32[2,128,64]{1,2,0:T(8,128)S(1)}) %tuple.202, (s32[]{:T(128)}, s32[2]{0:T(128)S(1)}, s32[2,1,1]{0,2,1:T(1,128)S(1)}, ...), branch_computations={%region_3.3_spmd, %region_4.4_spmd.clone} | conditional | flops 13465407 | bytes 2832748 | solution.py:159
  149.0 1.0 convolution_bitcast_fusion
  151.4 4.5 %conditional.4 = (f32[2,128,64]{1,2,0:T(8,128)S(1)}, f32[2,128,64]{1,2,0:T(8,128)S(1)}, f32[1,2,8,8,64]{2,3,4,1,0:T(8,128)S(1)}) conditional(s32[]{:T(128)} %convert_element_type.314, (f32[2,128,64]{1,2,0:T(8,128)S(1)}, f32[2,128,64]{1,2,0:T(8,128)S(1)}) %tuple.202, (s32[]{:T(128)}, s32[2]{0:T(128)S(1)}, s32[2,1,1]{0,2,1:T(1,128)S(1)}, ...), branch_computations={%region_3.3_spmd, %region_4.4_spmd.clone} | conditional | flops 13465407 | bytes 2832748 | solution.py:159
  154.9 1.0 convolution_bitcast_fusion
  157.4 4.5 %conditional.4 = (f32[2,128,64]{1,2,0:T(8,128)S(1)}, f32[2,128,64]{1,2,0:T(8,128)S(1)}, f32[1,2,8,8,64]{2,3,4,1,0:T(8,128)S(1)}) conditional(s32[]{:T(128)} %convert_element_type.314, (f32[2,128,64]{1,2,0:T(8,128)S(1)}, f32[2,128,64]{1,2,0:T(8,128)S(1)}) %tuple.202, (s32[]{:T(128)}, s32[2]{0:T(128)S(1)}, s32[2,1,1]{0,2,1:T(1,128)S(1)}, ...), branch_computations={%region_3.3_spmd, %region_4.4_spmd.clone} | conditional | flops 13465407 | bytes 2832748 | solution.py:159
  160.9 1.0 convolution_bitcast_fusion
  163.3 4.5 %conditional.4 = (f32[2,128,64]{1,2,0:T(8,128)S(1)}, f32[2,128,64]{1,2,0:T(8,128)S(1)}, f32[1,2,8,8,64]{2,3,4,1,0:T(8,128)S(1)}) conditional(s32[]{:T(128)} %convert_element_type.314, (f32[2,128,64]{1,2,0:T(8,128)S(1)}, f32[2,128,64]{1,2,0:T(8,128)S(1)}) %tuple.202, (s32[]{:T(128)}, s32[2]{0:T(128)S(1)}, s32[2,1,1]{0,2,1:T(1,128)S(1)}, ...), branch_computations={%region_3.3_spmd, %region_4.4_spmd.clone} | conditional | flops 13465407 | bytes 2832748 | solution.py:159
  166.9 1.0 convolution_bitcast_fusion
  169.3 4.5 %conditional.4 = (f32[2,128,64]{1,2,0:T(8,128)S(1)}, f32[2,128,64]{1,2,0:T(8,128)S(1)}, f32[1,2,8,8,64]{2,3,4,1,0:T(8,128)S(1)}) conditional(s32[]{:T(128)} %convert_element_type.314, (f32[2,128,64]{1,2,0:T(8,128)S(1)}, f32[2,128,64]{1,2,0:T(8,128)S(1)}) %tuple.202, (s32[]{:T(128)}, s32[2]{0:T(128)S(1)}, s32[2,1,1]{0,2,1:T(1,128)S(1)}, ...), branch_computations={%region_3.3_spmd, %region_4.4_spmd.clone} | conditional | flops 13465407 | bytes 2832748 | solution.py:159
  172.8 1.0 convolution_bitcast_fusion
  175.4 15.4 %all_to_all.10 = f32[64,1,256]{2,1,0:T(1,128)S(1)} all-to-all(f32[64,1,256]{2,1,0:T(1,128)S(1)} %reshape.2622), channel_id=1, replica_groups=mesh['beta'=64,'grp'=2] {'beta'}, dimensions={0} | all-to-all | bytes 131072 | tf_op jit(solution)/shard_map/all_to_all | solution.py:23
  192.4 0.8 pad_maximum_fusion
  (611 shorter events, 102.6 us)
Async XLA Ops:
  29.9 1.6 copy-start.57
  30.7 1.6 copy-start.56
  32.3 1.6 copy-start.54
  33.1 1.6 copy-start.53
  33.9 1.6 copy-start.52
  34.7 1.6 copy-start.51
  35.6 1.6 copy-start.50
  36.4 1.6 copy-start.49
  37.2 1.6 copy-start.48
  38.0 1.6 copy-start.47
  38.8 1.6 copy-start.46
  39.6 1.6 copy-start.45
  40.5 1.6 copy-start.44
  41.3 1.6 copy-start.43
  42.1 1.6 copy-start.42
  42.9 1.6 copy-start.41
  43.7 1.6 copy-start.40
  44.5 1.6 copy-start.39
  45.4 1.6 copy-start.38
  46.2 1.6 copy-start.37
  47.0 1.6 copy-start.36
  47.8 1.8 copy-start.35
  48.6 1.8 copy-start.34
  49.6 1.6 copy-start.33
  50.4 1.6 copy-start.32
  51.2 1.6 copy-start.31
  52.0 1.6 copy-start.30
  52.9 1.6 copy-start.29
  53.7 1.6 copy-start.28
  54.5 1.6 copy-start.27
  97.8 24.9 %all-to-all-start = ((f32[64,1,2048]{2,1,0:T(1,128)}), f32[64,1,2048]{2,1,0:T(1,128)S(1)}, u32[]{:S(2)}, u32[]{:S(2)}) async-start(f32[64,1,2048]{2,1,0:T(1,128)} %reshape.2620), calls=%async_computation | async-start | bytes 1048576 | tf_op jit(solution)/shard_map/all_to_all | solution.py:11
  174.2 18.2 %collective-permute-start = (f32[1,8,64,64]{3,2,1,0:T(8,128)S(1)}, f32[1,8,64,64]{3,2,1,0:T(8,128)S(1)}, u32[]{:S(2)}, u32[]{:S(2)}) collective-permute-start(f32[1,8,64,64]{3,2,1,0:T(8,128)S(1)} %get-tuple-element.575), channel_id=1, source_target_pairs={{0,64},{2,66},{4,68},{6,70},{8,72},{10,74},{12,76},{14,78},{16,80}... | collective-permute-start | bytes 393224 | tf_op jit(solution)/shard_map/ppermute | solution.py:18
  (67 other events, 59.2 us)
